TPU v7x, 32 devices: a whole 2x2x4 slice. The times are simulated.
32 devices in a mesh: slab: 16 (over z, y, x), sub: 2 (over core).
Axes of the slice: x: 2, y: 2, z: 4, core: 2. Of those that a mesh axis runs over, the one named last changes fastest.
Arguments:
- start: float32 [4, 96, 32, 256], P(None, 'slab', 'sub'), may hold values from -6 to 6
- wind: float32 [3, 96, 32, 256], P(None, 'slab', 'sub'), may hold values from -4 to 4
- reaction: float32 [96, 32, 256], P('slab', 'sub'), may hold values from 0.5 to 4
- mass: float32 [96, 32, 256], P('slab', 'sub'), may hold values from 0.5 to 2
Outputs:
- basis: float32 [4, 4, 96, 32, 256], P(None, None, 'slab', 'sub')
- search: float32 [3, 4, 96, 32, 256], P(None, None, 'slab', 'sub')
- hessenberg: float32 [4, 3], replicated
All inputs are finite; a program needn't handle non-finite values.
Results may differ from a plain program's by a relative error of at most 0.0003.
Values sent between devices are 32-bit elements; how exact they have to be, the bound alone decides.
A program may use at most 64 MiB of HBM per device.

v0:
```python
import jax
import jax.numpy as jnp
from jax import lax
from jax.sharding import PartitionSpec as P

ITERS = 3


def padded_2(shard, sides, width):
    for axis, dim in sides:
        devices, length = (lax.axis_size(axis), shard.shape[dim])
        up = [(i, (i + 1) % devices) for i in range(devices - 1)]
        down = [(j, i) for i, j in up]
        last = lax.slice_in_dim(shard, length - width, length, axis=dim)
        leading = lax.slice_in_dim(shard, 0, width, axis=dim)
        before = lax.ppermute(last, axis, up)
        after = lax.ppermute(leading, axis, down)
        shard = jnp.concatenate([before, shard, after], axis=dim)
    return shard


def neighbour_sets(padded):
    center = padded[..., 1:-1, 1:-1, :]
    zero_face = jnp.zeros_like(center[..., :1])
    plus_side = (
        padded[..., 2:, 1:-1, :],
        padded[..., 1:-1, 2:, :],
        jnp.concatenate([center[..., 1:], zero_face], -1),
    )
    minus_side = (
        padded[..., :-2, 1:-1, :],
        padded[..., 1:-1, :-2, :],
        jnp.concatenate([zero_face, center[..., :-1]], -1),
    )
    return (center, plus_side, minus_side)


def six_sum(plus_side, minus_side):
    total = plus_side[0] + minus_side[0]
    total = total + plus_side[1] + minus_side[1]
    return total + plus_side[2] + minus_side[2]


def transport(padded, reaction_k, wind_k):
    center, plus_side, minus_side = neighbour_sets(padded)
    convect = wind_k[0] * (plus_side[0] - minus_side[0])
    convect = convect + wind_k[1] * (plus_side[1] - minus_side[1])
    convect = convect + wind_k[2] * (plus_side[2] - minus_side[2])
    return (6.0 + reaction_k) * center - six_sum(plus_side, minus_side) + 0.5 * convect


def gradient(padded):
    center, plus_side, minus_side = neighbour_sets(padded)
    return jnp.stack(
        [0.5 * (plus_side[dim_index] - minus_side[dim_index]) for dim_index in range(3)]
    )


def divergence(padded):
    center, plus_side, minus_side = neighbour_sets(padded)
    total = 0.5 * (plus_side[0][0] - minus_side[0][0])
    total = total + 0.5 * (plus_side[1][1] - minus_side[1][1])
    return total + 0.5 * (plus_side[2][2] - minus_side[2][2])


def pressure_poisson(padded):
    center, plus_side, minus_side = neighbour_sets(padded)
    return 7.0 * center - six_sum(plus_side, minus_side)


def oseen_apply(padded, reaction_k, wind_k):
    upper = transport(padded[:3], reaction_k, wind_k) + gradient(padded[3])
    center, plus_side, minus_side = neighbour_sets(padded[3])
    lower = -divergence(padded[:3]) - 0.5 * (6.0 * center - six_sum(plus_side, minus_side))
    return jnp.concatenate([upper, lower[None]], 0)


def local_dots(vectors, image):
    return jnp.stack([jnp.sum(vector * image) for vector in vectors])


def per_device(start, wind, reaction, mass):
    cells_x = start.shape[1]
    cells_y = start.shape[2]

    def inside(width):
        global_x = (
            lax.axis_index("slab") * cells_x
            - width
            + jnp.arange(cells_x + 2 * width, dtype=jnp.int32)
        )
        global_y = (
            lax.axis_index("sub") * cells_y
            - width
            + jnp.arange(cells_y + 2 * width, dtype=jnp.int32)
        )
        inside_x = (global_x >= 0) & (global_x < cells_x * lax.axis_size("slab"))
        inside_y = (global_y >= 0) & (global_y < cells_y * lax.axis_size("sub"))
        return (inside_x[:, None] & inside_y[None, :])[:, :, None]

    stacked = jnp.concatenate([wind, reaction[None], mass[None]], 0)
    coeffs = padded_2(stacked, (("slab", 1), ("sub", 2)), 3)

    def coef_at(width):
        offset = 3 - width
        return coeffs[
            :, offset : offset + cells_x + 2 * width, offset : offset + cells_y + 2 * width, :
        ]

    def apply_both(vector):
        extended = padded_2(vector, (("slab", 1), ("sub", 2)), 5)
        pressure = extended[3]
        first_guess = pressure / 7.0
        second_guess = (
            first_guess[1:-1, 1:-1] + (pressure[1:-1, 1:-1] - pressure_poisson(first_guess)) / 7.0
        )
        second_guess = jnp.where(inside(4), second_guess, 0.0)
        coef_three = coef_at(3)
        schur = jnp.where(
            inside(3), -transport(second_guess, coef_three[3], coef_three[:3]) / coef_three[4], 0.0
        )
        residue = jnp.where(inside(2), extended[:3, 3:-3, 3:-3] - gradient(schur), 0.0)
        coef_two = coef_at(2)
        velocity_first = residue / (6.0 + coef_two[3])
        coef_one = coef_at(1)
        velocity = velocity_first[:, 1:-1, 1:-1] + (
            residue[:, 1:-1, 1:-1] - transport(velocity_first, coef_one[3], coef_one[:3])
        ) / (6.0 + coef_one[3])
        velocity = jnp.where(inside(1), velocity, 0.0)
        found = jnp.concatenate([velocity, schur[None, 2:-2, 2:-2]], 0)
        image = oseen_apply(found, reaction, wind)
        return (found[:, 1:-1, 1:-1], image)

    scale_start = jnp.sqrt(lax.psum(jnp.sum(start * start), ("slab", "sub")))
    vectors = [start / scale_start]
    first_found, first_image = apply_both(vectors[0])
    searches = [first_found]
    images = [first_image]
    hess = jnp.zeros((ITERS + 1, ITERS), jnp.float32)
    for column in range(ITERS):
        image = images[column]
        projected = lax.psum(local_dots(vectors, image), ("slab", "sub"))
        for row in range(column + 1):
            image = image - projected[row] * vectors[row]
        norm_next = jnp.sqrt(lax.psum(jnp.sum(image * image), ("slab", "sub")))
        hess = hess.at[: column + 1, column].set(projected)
        hess = hess.at[column + 1, column].set(norm_next)
        vectors.append(image / norm_next)
        if column + 1 < ITERS:
            next_found, next_image = apply_both(vectors[column + 1])
            searches.append(next_found)
            images.append(next_image)
    return (jnp.stack(vectors), jnp.stack(searches), hess)


def solution(mesh):
    return jax.shard_map(
        per_device,
        mesh=mesh,
        in_specs=(
            P(None, "slab", "sub", None),
            P(None, "slab", "sub", None),
            P("slab", "sub", None),
            P("slab", "sub", None),
        ),
        out_specs=(P(None, None, "slab", "sub", None), P(None, None, "slab", "sub", None), P()),
        check_vma=False,
    )
```

profile of v0, /device:TPU:0, one launch (start us, length us, event | category | flops | bytes accessed | tf_op | source)
XLA Modules:
  0.0 415.6 jit_solution(4579641855387996888)
XLA Ops:
  2.5 5.0 %collective-permute-start.4 = (f32[5,3,16,256]{3,2,1,0:T(8,128)}, f32[5,3,16,256]{3,2,1,0:T(8,128)S(1)}, u32[]{:S(2)}, u32[]{:S(2)}) collective-permute-start(f32[5,3,16,256]{3,2,1,0:T(8,128)} %get-tuple-element.129), channel_id=1, source_target_pairs={{0,2},{2,4},{4,6},{6,8},{8,10},{10,12},{12,14},{14,16},{16,18},{18... | collective-permute-start | bytes 737288 | tf_op jit(solution)/shard_map/ppermute | solution.py:16
  8.3 1.4 collective-permute-start.5
  9.7 44.7 %psum.49 = f32[]{:T(128)} all-reduce(f32[]{:T(128)} %multiply_reduce_fusion.9), channel_id=1, replica_groups=mesh['slab'=16,'sub'=2] {'slab','sub'}, use_global_device_ids=true, to_apply=%region_1.0 | all-reduce | flops 1 | bytes 8 | tf_op jit(solution)/shard_map/psum | solution.py:134
  55.2 4.2 %collective-permute-start = (f32[4,5,16,256]{3,2,1,0:T(8,128)S(1)}, f32[4,5,16,256]{3,2,1,0:T(8,128)S(1)}, u32[]{:S(2)}, u32[]{:S(2)}) collective-permute-start(f32[4,5,16,256]{3,2,1,0:T(8,128)S(1)} %get-tuple-element.135), channel_id=1, source_target_pairs={{0,2},{2,4},{4,6},{6,8},{8,10},{10,12},{12,14},{14,16},{16,18},{18... | collective-permute-start | bytes 983048 | tf_op jit(solution)/shard_map/ppermute | solution.py:16
  66.0 6.1 %collective-permute-done = f32[4,5,16,256]{3,2,1,0:T(8,128)S(1)} collective-permute-done((f32[4,5,16,256]{3,2,1,0:T(8,128)S(1)}, f32[4,5,16,256]{3,2,1,0:T(8,128)S(1)}, u32[]{:S(2)}, u32[]{:S(2)}) %collective-permute-start) | collective-permute-done | bytes 327712 | tf_op jit(solution)/shard_map/ppermute | solution.py:16
  72.1 1.9 collective-permute-done.1
  74.2 1.5 collective-permute-start.2
  77.4 2.0 collective-permute-done.3
  83.6 38.5 %psum.50 = f32[1]{0:T(128)} all-reduce(f32[1]{0:T(128)} %bitcast.25), channel_id=1, replica_groups=mesh['slab'=16,'sub'=2] {'slab','sub'}, use_global_device_ids=true, to_apply=%region_3.4 | all-reduce | flops 1 | bytes 8 | tf_op jit(solution)/shard_map/psum | solution.py:142
  124.1 41.0 %psum.51 = f32[]{:T(128)} all-reduce(f32[]{:T(128)} %multiply_reduce_fusion.7), channel_id=1, replica_groups=mesh['slab'=16,'sub'=2] {'slab','sub'}, use_global_device_ids=true, to_apply=%region_5.6 | all-reduce | flops 1 | bytes 8 | tf_op jit(solution)/shard_map/psum | solution.py:145
  165.8 1.6 broadcast_divide_fusion.4
  167.5 4.2 %collective-permute-start.8 = (f32[4,5,16,256]{3,2,1,0:T(8,128)S(1)}, f32[4,5,16,256]{3,2,1,0:T(8,128)S(1)}, u32[]{:S(2)}, u32[]{:S(2)}) collective-permute-start(f32[4,5,16,256]{3,2,1,0:T(8,128)S(1)} %get-tuple-element.133), channel_id=1, source_target_pairs={{0,2},{2,4},{4,6},{6,8},{8,10},{10,12},{12,14},{14,16},{16,18},{18... | collective-permute-start | bytes 983048 | tf_op jit(solution)/shard_map/ppermute | solution.py:16
  176.3 8.0 %collective-permute-done.8 = f32[4,5,16,256]{3,2,1,0:T(8,128)S(1)} collective-permute-done((f32[4,5,16,256]{3,2,1,0:T(8,128)S(1)}, f32[4,5,16,256]{3,2,1,0:T(8,128)S(1)}, u32[]{:S(2)}, u32[]{:S(2)}) %collective-permute-start.8) | collective-permute-done | bytes 327712 | tf_op jit(solution)/shard_map/ppermute | solution.py:16
  184.3 1.9 collective-permute-done.9
  187.7 1.5 collective-permute-start.11
  190.0 1.5 collective-permute-done.11
  199.3 1.4 scatter.21
  200.7 38.9 %psum.52 = f32[2]{0:T(128)S(1)} all-reduce(f32[2]{0:T(128)S(1)} %pad_maximum_fusion.30), channel_id=1, replica_groups=mesh['slab'=16,'sub'=2] {'slab','sub'}, use_global_device_ids=true, to_apply=%region_8.9 | all-reduce | flops 2 | bytes 16 | tf_op jit(solution)/shard_map/psum | solution.py:142
  240.3 3.6 multiply_reduce_fusion.4
  243.9 40.7 %psum.53 = f32[]{:T(128)} all-reduce(f32[]{:T(128)} %get-tuple-element.89), channel_id=1, replica_groups=mesh['slab'=16,'sub'=2] {'slab','sub'}, use_global_device_ids=true, to_apply=%region_10.11 | all-reduce | flops 1 | bytes 8 | tf_op jit(solution)/shard_map/psum | solution.py:145
  287.3 4.9 %collective-permute-start.12 = (f32[4,5,16,256]{3,2,1,0:T(8,128)}, f32[4,5,16,256]{3,2,1,0:T(8,128)}, u32[]{:S(2)}, u32[]{:S(2)}) collective-permute-start(f32[4,5,16,256]{3,2,1,0:T(8,128)} %get-tuple-element.131), channel_id=1, source_target_pairs={{0,2},{2,4},{4,6},{6,8},{8,10},{10,12},{12,14},{14,16},{16,18},{18... | collective-permute-start | bytes 983048 | tf_op jit(solution)/shard_map/ppermute | solution.py:16
  293.6 3.1 broadcast_select_fusion.1
  296.7 2.6 scatter.24
  299.3 1.4 scatter.25
  300.6 3.3 collective-permute-done.12
  303.9 1.9 collective-permute-done.13
  310.7 1.6 collective-permute-done.15
  320.7 2.0 pad_maximum_fusion.31
  322.8 39.6 %psum.54 = f32[3]{0:T(128)S(1)} all-reduce(f32[3]{0:T(128)S(1)} %pad_maximum_fusion.31), channel_id=1, replica_groups=mesh['slab'=16,'sub'=2] {'slab','sub'}, use_global_device_ids=true, to_apply=%region_14.15 | all-reduce | flops 3 | bytes 24 | tf_op jit(solution)/shard_map/psum | solution.py:142
  363.1 1.9 broadcast_select_fusion
  366.3 3.5 multiply_reduce_fusion
  369.8 40.8 %psum.55 = f32[]{:T(128)} all-reduce(f32[]{:T(128)} %get-tuple-element.83), channel_id=1, replica_groups=mesh['slab'=16,'sub'=2] {'slab','sub'}, use_global_device_ids=true, to_apply=%region_16.17 | all-reduce | flops 1 | bytes 8 | tf_op jit(solution)/shard_map/psum | solution.py:145
  (210 shorter events, 54.8 us)
Async XLA Ops:
  2.5 58.8 %copy-start.31 = (f32[6,16,256]{2,1,0:T(8,128)S(1)}, f32[6,16,256]{2,1,0:T(8,128)}, u32[]{:S(2)}) copy-start(f32[6,16,256]{2,1,0:T(8,128)} %param.18) | copy-start | bytes 294916
  2.5 58.8 %copy-start.3 = (f32[3,6,16,256]{3,2,1,0:T(8,128)S(1)}, f32[3,6,16,256]{3,2,1,0:T(8,128)}, u32[]{:S(2)}) copy-start(f32[3,6,16,256]{3,2,1,0:T(8,128)} %param.17) | copy-start | bytes 884740
  2.5 60.7 %collective-permute-start.4 = (f32[5,3,16,256]{3,2,1,0:T(8,128)}, f32[5,3,16,256]{3,2,1,0:T(8,128)S(1)}, u32[]{:S(2)}, u32[]{:S(2)}) collective-permute-start(f32[5,3,16,256]{3,2,1,0:T(8,128)} %get-tuple-element.129), channel_id=1, source_target_pairs={{0,2},{2,4},{4,6},{6,8},{8,10},{10,12},{12,14},{14,16},{16,18},{18... | collective-permute-start | bytes 737288 | tf_op jit(solution)/shard_map/ppermute | solution.py:16
  8.3 53.3 %copy-start.44 = (s32[2]{0:T(128)S(1)}, s32[2]{0:T(128)}, u32[]{:S(2)}) copy-start(s32[2]{0:T(128)} %constant.231.clone.1) | copy-start | bytes 28
  8.3 55.0 %collective-permute-start.5 = (f32[5,3,16,256]{3,2,1,0:T(8,128)S(1)}, f32[5,3,16,256]{3,2,1,0:T(8,128)S(1)}, u32[]{:S(2)}, u32[]{:S(2)}) collective-permute-start(f32[5,3,16,256]{3,2,1,0:T(8,128)S(1)} %get-tuple-element.130), channel_id=1, source_target_pairs={{2,0},{4,2},{6,4},{8,6},{10,8},{12,10},{14,12},{16,14},{18,16},{20... | collective-permute-start | bytes 737288 | tf_op jit(solution)/shard_map/ppermute | solution.py:17
  55.2 16.8 %collective-permute-start = (f32[4,5,16,256]{3,2,1,0:T(8,128)S(1)}, f32[4,5,16,256]{3,2,1,0:T(8,128)S(1)}, u32[]{:S(2)}, u32[]{:S(2)}) collective-permute-start(f32[4,5,16,256]{3,2,1,0:T(8,128)S(1)} %get-tuple-element.135), channel_id=1, source_target_pairs={{0,2},{2,4},{4,6},{6,8},{8,10},{10,12},{12,14},{14,16},{16,18},{18... | collective-permute-start | bytes 983048 | tf_op jit(solution)/shard_map/ppermute | solution.py:16
  59.4 14.5 %collective-permute-start.1 = (f32[4,5,16,256]{3,2,1,0:T(8,128)S(1)}, f32[4,5,16,256]{3,2,1,0:T(8,128)S(1)}, u32[]{:S(2)}, u32[]{:S(2)}) collective-permute-start(f32[4,5,16,256]{3,2,1,0:T(8,128)S(1)} %get-tuple-element.136), channel_id=1, source_target_pairs={{2,0},{4,2},{6,4},{8,6},{10,8},{12,10},{14,12},{16,14},{18,16},{20... | collective-permute-start | bytes 983048 | tf_op jit(solution)/shard_map/ppermute | solution.py:17
  61.3 134.9 %copy-start.19 = (f32[6,16,256]{2,1,0:T(8,128)}, f32[6,16,256]{2,1,0:T(8,128)S(1)}, u32[]{:S(2)}) copy-start(f32[6,16,256]{2,1,0:T(8,128)S(1)} %broadcast_add_fusion) | copy-start | bytes 294916
  61.4 21.2 %copy-start.21 = (f32[6,16,256]{2,1,0:T(8,128)}, f32[6,16,256]{2,1,0:T(8,128)S(1)}, u32[]{:S(2)}) copy-start(f32[6,16,256]{2,1,0:T(8,128)S(1)} %get-tuple-element.161) | copy-start | bytes 294916
  61.4 21.2 %copy-start.24 = (f32[6,16,256]{2,1,0:T(8,128)}, f32[6,16,256]{2,1,0:T(8,128)S(1)}, u32[]{:S(2)}) copy-start(f32[6,16,256]{2,1,0:T(8,128)S(1)} %get-tuple-element.162) | copy-start | bytes 294916
  61.4 21.2 %copy-start.27 = (f32[6,16,256]{2,1,0:T(8,128)}, f32[6,16,256]{2,1,0:T(8,128)S(1)}, u32[]{:S(2)}) copy-start(f32[6,16,256]{2,1,0:T(8,128)S(1)} %get-tuple-element.163) | copy-start | bytes 294916
  63.2 8.8 %copy-start.35 = (f32[5,3,16,256]{3,2,1,0:T(8,128)}, f32[5,3,16,256]{3,2,1,0:T(8,128)S(1)}, u32[]{:S(2)}) copy-start(f32[5,3,16,256]{3,2,1,0:T(8,128)S(1)} %collective-permute-done.4) | copy-start | bytes 737284
  63.2 8.8 %copy-start.37 = (f32[5,3,16,256]{3,2,1,0:T(8,128)}, f32[5,3,16,256]{3,2,1,0:T(8,128)S(1)}, u32[]{:S(2)}) copy-start(f32[5,3,16,256]{3,2,1,0:T(8,128)S(1)} %collective-permute-done.5) | copy-start | bytes 737284
  63.3 13.6 %collective-permute-start.6 = (f32[5,12,3,256]{3,2,1,0:T(4,128)S(1)}, f32[5,12,3,256]{3,2,1,0:T(4,128)S(1)}, u32[]{:S(2)}, u32[]{:S(2)}) collective-permute-start(f32[5,12,3,256]{3,2,1,0:T(4,128)S(1)} %get-tuple-element.109), channel_id=1, source_target_pairs={{0,1},{2,3},{4,5},{6,7},{8,9},{10,11},{12,13},{14,15},{16,17},{18,... | collective-permute-start | bytes 552968 | tf_op jit(solution)/shard_map/ppermute | solution.py:16
  64.7 12.3 %collective-permute-start.7 = (f32[5,12,3,256]{3,2,1,0:T(4,128)S(1)}, f32[5,12,3,256]{3,2,1,0:T(4,128)S(1)}, u32[]{:S(2)}, u32[]{:S(2)}) collective-permute-start(f32[5,12,3,256]{3,2,1,0:T(4,128)S(1)} %get-tuple-element.110), channel_id=1, source_target_pairs={{1,0},{3,2},{5,4},{7,6},{9,8},{11,10},{13,12},{15,14},{17,16},{19,... | collective-permute-start | bytes 552968 | tf_op jit(solution)/shard_map/ppermute | solution.py:17
  74.2 3.2 collective-permute-start.2
  75.7 3.8 collective-permute-start.3
  82.5 82.5 %copy-start.30 = (f32[1,6,16,256]{3,2,1,0:T(8,128)}, f32[1,6,16,256]{3,2,1,0:T(8,128)S(1)}, u32[]{:S(2)}) copy-start(f32[1,6,16,256]{3,2,1,0:T(8,128)S(1)} %get-tuple-element.166) | copy-start | bytes 294916
  167.5 16.8 %collective-permute-start.8 = (f32[4,5,16,256]{3,2,1,0:T(8,128)S(1)}, f32[4,5,16,256]{3,2,1,0:T(8,128)S(1)}, u32[]{:S(2)}, u32[]{:S(2)}) collective-permute-start(f32[4,5,16,256]{3,2,1,0:T(8,128)S(1)} %get-tuple-element.133), channel_id=1, source_target_pairs={{0,2},{2,4},{4,6},{6,8},{8,10},{10,12},{12,14},{14,16},{16,18},{18... | collective-permute-start | bytes 983048 | tf_op jit(solution)/shard_map/ppermute | solution.py:16
  171.7 14.5 %collective-permute-start.9 = (f32[4,5,16,256]{3,2,1,0:T(8,128)S(1)}, f32[4,5,16,256]{3,2,1,0:T(8,128)S(1)}, u32[]{:S(2)}, u32[]{:S(2)}) collective-permute-start(f32[4,5,16,256]{3,2,1,0:T(8,128)S(1)} %get-tuple-element.134), channel_id=1, source_target_pairs={{2,0},{4,2},{6,4},{8,6},{10,8},{12,10},{14,12},{16,14},{18,16},{20... | collective-permute-start | bytes 983048 | tf_op jit(solution)/shard_map/ppermute | solution.py:17
  186.4 3.7 collective-permute-start.10
  187.7 3.8 collective-permute-start.11
  239.6 45.7 %copy-start.42 = (f32[2]{0:T(128)}, f32[2]{0:T(128)S(1)}, u32[]{:S(2)}) copy-start(f32[2]{0:T(128)S(1)} %psum.52) | copy-start | bytes 28
  285.3 8.2 %copy-start.43 = (f32[2]{0:T(128)S(1)}, f32[2]{0:T(128)}, u32[]{:S(2)}) copy-start(f32[2]{0:T(128)} %copy-done.42) | copy-start | bytes 28
  287.3 16.6 %collective-permute-start.12 = (f32[4,5,16,256]{3,2,1,0:T(8,128)}, f32[4,5,16,256]{3,2,1,0:T(8,128)}, u32[]{:S(2)}, u32[]{:S(2)}) collective-permute-start(f32[4,5,16,256]{3,2,1,0:T(8,128)} %get-tuple-element.131), channel_id=1, source_target_pairs={{0,2},{2,4},{4,6},{6,8},{8,10},{10,12},{12,14},{14,16},{16,18},{18... | collective-permute-start | bytes 983048 | tf_op jit(solution)/shard_map/ppermute | solution.py:16
  292.3 13.6 %collective-permute-start.13 = (f32[4,5,16,256]{3,2,1,0:T(8,128)}, f32[4,5,16,256]{3,2,1,0:T(8,128)}, u32[]{:S(2)}, u32[]{:S(2)}) collective-permute-start(f32[4,5,16,256]{3,2,1,0:T(8,128)} %get-tuple-element.132), channel_id=1, source_target_pairs={{2,0},{4,2},{6,4},{8,6},{10,8},{12,10},{14,12},{16,14},{18,16},{20... | collective-permute-start | bytes 983048 | tf_op jit(solution)/shard_map/ppermute | solution.py:17
  307.2 3.5 collective-permute-start.14
  308.5 3.8 collective-permute-start.15
  319.9 43.2 %copy-start.41 = (f32[4,3]{0,1:T(4,128)S(1)}, f32[4,3]{0,1:T(4,128)}, u32[]{:S(2)}) copy-start(f32[4,3]{0,1:T(4,128)} %scatter.25) | copy-start | bytes 148
  319.9 46.4 %copy-start.2 = (f32[4,6,16,256]{3,2,1,0:T(8,128)S(1)}, f32[4,6,16,256]{3,2,1,0:T(8,128)}, u32[]{:S(2)}) copy-start(f32[4,6,16,256]{3,2,1,0:T(8,128)} %get-tuple-element.90) | copy-start | bytes 1179652
  322.8 90.4 %copy-start.33 = (f32[1,4,6,16,256]{4,3,2,1,0:T(8,128)S(1)}, f32[1,4,6,16,256]{4,3,2,1,0:T(8,128)}, u32[]{:S(2)}) copy-start(f32[1,4,6,16,256]{4,3,2,1,0:T(8,128)} %fusion.17) | copy-start | bytes 1179652
  322.8 90.4 %copy-start.34 = (f32[1,4,6,16,256]{4,3,2,1,0:T(8,128)S(1)}, f32[1,4,6,16,256]{4,3,2,1,0:T(8,128)}, u32[]{:S(2)}) copy-start(f32[1,4,6,16,256]{4,3,2,1,0:T(8,128)} %fusion.16) | copy-start | bytes 1179652
  (29 other events, 65.5 us)
where the time goes:
time: 418 us; the launch traced here: 416 us
  blocking collectives  284 us (68%)
  other arithmetic  42.8 us (10%)
  starting transfers between devices  34.4 us (8%)
  waiting for transfers between devices  28.3 us (7%)
  local copies, waits for them, and re-layouts  21.4 us (5%)
  between operations  4.57 us (1%)
    psum x3, blocking collectives, per_device(): norm_next = jnp.sqrt(lax.psum(jnp.sum(image * image), ('slab', 'sub')))  122 us
    psum x3, blocking collectives, per_device(): projected = lax.psum(local_dots(vectors, image), ('slab', 'sub'))  117 us
    psum x1, blocking collectives, per_device(): scale_start = jnp.sqrt(lax.psum(jnp.sum(start * start), ('slab', 'sub')))  44.7 us
    ppermute x8, starting transfers between devices, padded_2(): before = lax.ppermute(last, axis, up)  23.7 us
    ppermute x8, waiting for transfers between devices, padded_2(): before = lax.ppermute(last, axis, up)  17.4 us
    ppermute x8, waiting for transfers between devices, padded_2(): after = lax.ppermute(leading, axis, down)  10.9 us
    ppermute x8, starting transfers between devices, padded_2(): after = lax.ppermute(leading, axis, down)  10.6 us
    reduce_sum x3, other arithmetic, per_device(): norm_next = jnp.sqrt(lax.psum(jnp.sum(image * image), ('slab', 'sub')))  8.42 us
  transfers between devices with their start and end apart: 16, of which 9 were waited for; matrix products, arithmetic and copies ran while one was open for 4% of the time, Pallas kernels for 0%

commit v1 on v0

v1 whole, which is shorter than its diff:
```python
import functools

import jax
import jax.numpy as jnp
from jax import lax
from jax.experimental import pallas as pl
from jax.experimental.pallas import tpu as pltpu
from jax.sharding import PartitionSpec as P

ITERS = 3
WP, WU, WC = 5, 2, 3
HALO = 8
LANES = 128
MESH = pl.DeviceIdType.MESH


def fold(x):
    rows, cols = x.shape
    total = None
    for r in range(0, rows, 8):
        for c in range(0, cols, LANES):
            piece = x[r : r + 8, c : c + LANES]
            total = piece if total is None else total + piece
    return total


def kernel(
    slabs, subs, cx, cy, nz,
    start, wind, reaction, mass, basis, search, hess,
    xp, xu, vp, vu, raw, co, mk, t1, qq, y0, y1, wl, ob, os_, red,
    send, recv, red_send, red_recv, load, store,
):
    slab, sub = lax.axis_index("slab"), lax.axis_index("sub")
    n = slabs * subs
    me = slab * subs + sub
    rows = cy + HALO
    has_left, has_right = slab > 0, slab < slabs - 1

    loads = [
        pltpu.make_async_copy(start.at[3], xp.at[0, pl.ds(WP, cx), pl.ds(0, cy)], load.at[0]),
        pltpu.make_async_copy(
            start.at[pl.ds(0, 3)], xu.at[0, :, pl.ds(WU, cx), pl.ds(0, cy)], load.at[1]
        ),
        pltpu.make_async_copy(
            wind, raw.at[pl.ds(0, 3), pl.ds(WC, cx), pl.ds(0, cy)], load.at[2]
        ),
        pltpu.make_async_copy(reaction, raw.at[3, pl.ds(WC, cx), pl.ds(0, cy)], load.at[3]),
        pltpu.make_async_copy(mass, raw.at[4, pl.ds(WC, cx), pl.ds(0, cy)], load.at[4]),
    ]
    for item in loads:
        item.start()

    barrier = pltpu.get_barrier_semaphore()

    def greet(k, carry):
        other = lax.rem(me + k, n)
        pl.semaphore_signal(
            barrier, inc=1, device_id=(other // subs, other % subs), device_id_type=MESH
        )
        return carry

    lax.fori_loop(1, n, greet, 0)

    def clear(low):
        def inner():
            for e in range(ITERS):
                for k in range(WP):
                    at = k if low else WP + cx + k
                    xp[e, at, 0:cy] = jnp.zeros((cy, nz), jnp.float32)
                for c in range(3):
                    for k in range(WU):
                        at = k if low else WU + cx + k
                        xu[e, c, at, 0:cy] = jnp.zeros((cy, nz), jnp.float32)
            for c in range(5):
                for k in range(WC):
                    at = k if low else WC + cx + k
                    raw[c, at, 0:cy] = jnp.zeros((cy, nz), jnp.float32)
        return inner

    pl.when(jnp.logical_not(has_left))(clear(True))
    pl.when(jnp.logical_not(has_right))(clear(False))

    row = lax.broadcasted_iota(jnp.int32, (rows, nz), 0)
    col = lax.broadcasted_iota(jnp.int32, (rows, nz), 1)
    last = jnp.where(sub == 0, rows - 1, cy - 1)
    first = jnp.where(sub == 0, 0, cy)
    mk[0] = jnp.where(row == last, 0.0, 1.0)
    mk[1] = jnp.where(row == first, 0.0, 1.0)
    mk[2] = jnp.where(col == nz - 1, 0.0, 1.0)
    mk[3] = jnp.where(col == 0, 0.0, 1.0)

    pl.semaphore_wait(barrier, n - 1)

    def p_view(e):
        return lambda planes, lines: xp.at[e, planes, lines]

    def u_view(e):
        return lambda planes, lines: xu.at[e, :, planes, lines]

    def c_view(planes, lines):
        return raw.at[:, planes, lines]

    groups = [
        (p_view(0), WP), (u_view(0), WU), (c_view, WC),
        (p_view(1), WP), (u_view(1), WU), (p_view(2), WP), (u_view(2), WU),
    ]
    own_lines = pl.ds(0, cy)
    edge_lines = pl.ds(pl.multiple_of((1 - sub) * (cy - HALO), 8), HALO)
    halo_lines = pl.ds(cy, HALO)

    def remote(g, kind):
        view, w = groups[g]
        if kind == 0:
            src, dst = view(pl.ds(cx, w), own_lines), view(pl.ds(0, w), own_lines)
            target = {"slab": slab + 1}
        elif kind == 1:
            src, dst = view(pl.ds(w, w), own_lines), view(pl.ds(w + cx, w), own_lines)
            target = {"slab": slab - 1}
        else:
            planes = (pl.ds(w, cx), pl.ds(0, w), pl.ds(w + cx, w))[kind - 2]
            src, dst = view(planes, edge_lines), view(planes, halo_lines)
            target = {"sub": 1 - sub}
        return pltpu.make_async_remote_copy(
            src_ref=src, dst_ref=dst, send_sem=send.at[g, kind], recv_sem=recv.at[g, kind],
            device_id=target, device_id_type=MESH,
        )

    def begin(g):
        pl.when(has_right)(lambda: remote(g, 0).start())
        pl.when(has_left)(lambda: remote(g, 1).start())
        remote(g, 2).start()

    def forward(g):
        pl.when(has_left)(lambda: remote(g, 0).wait_recv())
        remote(g, 3).start()
        pl.when(has_right)(lambda: remote(g, 1).wait_recv())
        remote(g, 4).start()

    def arrive(g):
        for kind in (2, 3, 4):
            remote(g, kind).wait_recv()

    def finish(g):
        pl.when(has_right)(lambda: remote(g, 0).wait_send())
        pl.when(has_left)(lambda: remote(g, 1).wait_send())
        for kind in (2, 3, 4):
            remote(g, kind).wait_send()

    lane = lax.broadcasted_iota(jnp.int32, (1, LANES), 1)

    def reduce_start(e, parts):
        line = jnp.zeros((1, LANES), jnp.float32)
        for i, part in enumerate(parts):
            line = line + jnp.where(lane == i, jnp.sum(fold(part), keepdims=True), 0.0)
        red[e, me] = line

        def push(k, carry):
            other = lax.rem(me + k, n)
            pltpu.make_async_remote_copy(
                src_ref=red.at[e, me], dst_ref=red.at[e, me],
                send_sem=red_send.at[e], recv_sem=red_recv.at[e],
                device_id=(other // subs, other % subs), device_id_type=MESH,
            ).start()
            return carry

        lax.fori_loop(1, n, push, 0)

    def red_wait(e, sem):
        block = red.at[e, pl.ds(0, n - 1)]
        pltpu.make_async_copy(block, block, sem.at[e]).wait()

    def reduce_end(e, count):
        red_wait(e, red_recv)
        total = jnp.sum(red[e], axis=0)
        return [
            jnp.sum(jnp.where(lane == i, total, 0.0), axis=1, keepdims=True)
            for i in range(count)
        ]

    def turn(f):
        return (
            pltpu.roll(f, rows - 1, 0), pltpu.roll(f, 1, 0),
            pltpu.roll(f, nz - 1, 1), pltpu.roll(f, 1, 1),
        )

    def masked(f):
        yp, ym, zp, zm = turn(f)
        return yp * mk[0], ym * mk[1], zp * mk[2], zm * mk[3]

    def off_diagonal(below, around, above, k):
        yp, ym, zp, zm = around
        total = co[0, k] * above + co[1, k] * below
        total = total + (co[2, k] * yp + co[3, k] * ym)
        return total + (co[4, k] * zp + co[5, k] * zm)

    def loop(count, body, init=0):
        return lax.fori_loop(0, count, body, init)

    def inside(k, w):
        at = slab * cx + k - w
        return jnp.logical_and(at >= 0, at < slabs * cx)

    def coefficients():
        def body(k, carry):
            ok = jnp.where(inside(k, WC), 1.0, 0.0)
            keep = jnp.full((rows, nz), ok) > 0.5
            hx, hy, hz = 0.5 * raw[0, k], 0.5 * raw[1, k], 0.5 * raw[2, k]
            co[0, k] = 1.0 - hx
            co[1, k] = 1.0 + hx
            co[2, k] = (1.0 - hy) * mk[0]
            co[3, k] = (1.0 + hy) * mk[1]
            co[4, k] = (1.0 - hz) * mk[2]
            co[5, k] = (1.0 + hz) * mk[3]
            diagonal = 6.0 + raw[3, k]
            co[6, k] = diagonal
            co[7, k] = jnp.where(keep, 1.0 / diagonal, 0.0)
            co[8, k] = jnp.where(keep, 1.0 / raw[4, k], 0.0)
            return carry

        loop(cx + 2 * WC, body)

    def first_guess(p):
        def body(k, carry):
            here = p[k + 1]
            yp, ym, zp, zm = masked(here)
            total = (p[k] + p[k + 2]) + (yp + ym) + (zp + zm)
            ok = jnp.where(inside(k, WP - 1), 1.0 / 7.0, 0.0)
            t1[k] = (here + total * (1.0 / 7.0)) * ok
            return carry

        loop(cx + 2 * (WP - 1), body)

    def schur():
        def body(k, carry):
            here = t1[k + 1]
            off = off_diagonal(t1[k], turn(here), t1[k + 2], k)
            qq[k] = (off - co[6, k] * here) * co[8, k]
            return carry

        loop(cx + 2 * WC, body)

    def velocity_first(u):
        def body(k, carry):
            yp, ym, zp, zm = masked(qq[k + 1])
            scale = co[7, k + 1]
            y0[0, k] = (u[0, k] - 0.5 * (qq[k + 2] - qq[k])) * scale
            y0[1, k] = (u[1, k] - 0.5 * (yp - ym)) * scale
            y0[2, k] = (u[2, k] - 0.5 * (zp - zm)) * scale
            return carry

        loop(cx + 2 * WU, body)

    def velocity_second():
        def body(k, carry):
            scale = co[7, k + 2]
            for c in range(3):
                here = y0[c, k + 1]
                off = off_diagonal(y0[c, k], turn(here), y0[c, k + 2], k + 2)
                y1[c, k] = here + off * scale
            return carry

        loop(cx + 2, body)

    def image(e, vectors):
        def body(k, acc):
            q = qq[k + WC]
            qa, qb = qq[k + WC + 1], qq[k + WC - 1]
            yp, ym, zp, zm = masked(q)
            grads = (0.5 * (qa - qb), 0.5 * (yp - ym), 0.5 * (zp - zm))
            low = 0.5 * ((qa + qb) + (yp + ym) + (zp + zm)) - 3.0 * q
            out = []
            for c in range(3):
                here = y1[c, k + 1]
                below, above = y1[c, k], y1[c, k + 2]
                around = turn(here)
                off = off_diagonal(below, around, above, k + WC)
                w = (co[6, k + WC] * here - off + grads[c])[:cy]
                if c == 0:
                    low = low - 0.5 * (above - below)
                elif c == 1:
                    low = low - 0.5 * (around[0] * mk[0] - around[1] * mk[1])
                else:
                    low = low - 0.5 * (around[2] * mk[2] - around[3] * mk[3])
                os_[e, c, k] = here[:cy]
                out.append(w)
            os_[e, 3, k] = q[:cy]
            out.append(low[:cy])
            if e + 1 < ITERS:
                for c in range(3):
                    xu[e + 1, c, k + WU, 0:cy] = out[c]
                xp[e + 1, k + WP, 0:cy] = out[3]
            else:
                for c in range(4):
                    wl[c, k] = out[c]
            acc = list(acc)
            for i, (p, u) in enumerate(vectors):
                held = [u[c, k + WU, 0:cy] for c in range(3)] + [p[k + WP, 0:cy]]
                term = held[0] * out[0] + held[1] * out[1]
                acc[i + 1] = acc[i + 1] + (term + (held[2] * out[2] + held[3] * out[3]))
                if i == e:
                    term = held[0] * held[0] + held[1] * held[1]
                    acc[0] = acc[0] + (term + (held[2] * held[2] + held[3] * held[3]))
            return tuple(acc)

        zero = jnp.zeros((cy, nz), jnp.float32)
        return loop(cx, body, (zero,) * (e + 2))

    def write_out(e):
        return (
            pltpu.make_async_copy(ob.at[e], basis.at[e], store.at[0, e]),
            pltpu.make_async_copy(os_.at[e], search.at[e], store.at[1, e]),
        )

    def results(e, vector, inverse):
        p, u = vector

        def body(k, carry):
            for c in range(3):
                ob[e, c, k] = u[c, k + WU, 0:cy] * inverse
            ob[e, 3, k] = p[k + WP, 0:cy] * inverse
            for c in range(4):
                os_[e, c, k] = os_[e, c, k] * inverse
            return carry

        loop(cx, body)
        for item in write_out(e):
            item.start()

    loads[0].wait()
    begin(0)
    for item in loads[2:]:
        item.wait()
    begin(2)
    loads[1].wait()
    begin(1)
    forward(0)
    arrive(0)

    vectors = [(xp.at[0], xu.at[0])]
    inverses = []
    entries = {}
    first_guess(vectors[0][0])
    forward(2)
    arrive(2)
    coefficients()
    for e in range(ITERS):
        p, u = vectors[e]
        p_group, u_group = ((0, 1), (3, 4), (5, 6))[e]
        if e > 0:
            first_guess(p)
        schur()
        if e == 0:
            forward(u_group)
            arrive(u_group)
        else:
            forward(u_group)
            arrive(u_group)

            def form_u(k, carry, e=e):
                for c in range(3):
                    total = xu[e, c, k] * factor
                    for g, (_, other) in zip(weights, vectors[:e]):
                        total = total - g * other[c, k]
                    u[c, k] = total
                return carry

            loop(cx + 2 * WU, form_u)
        velocity_first(u)
        velocity_second()
        acc = image(e, vectors)
        reduce_start(e, acc)
        if e + 1 < ITERS:
            begin(p_group + 3 if e == 0 else 5)
            begin(u_group + 3 if e == 0 else 6)
        sums = reduce_end(e, e + 2)
        norm = jnp.sqrt(sums[0])
        factor = 1.0 / norm
        if e > 0:
            entries[(e, e - 1)] = norm
        inverses.append(factor)
        weights = []
        for i in range(e + 1):
            h = sums[i + 1] * inverses[i] * factor
            entries[(i, e)] = h
            weights.append(h * inverses[i])
        results(e, vectors[e], factor)
        if e + 1 < ITERS:
            g_p = (3, 5)[e]
            forward(g_p)
            arrive(g_p)
            new = (vp.at[e], vu.at[e])

            def form_p(k, carry, e=e):
                total = xp[e + 1, k] * factor
                for g, (other, _) in zip(weights, vectors[: e + 1]):
                    total = total - g * other[k]
                vp[e, k] = total
                return carry

            loop(cx + 2 * WP, form_p)
            vectors.append(new)

    def close(k, acc):
        for c in range(4):
            total = wl[c, k] * factor
            for g, (p, u) in zip(weights, vectors):
                held = p[k + WP, 0:cy] if c == 3 else u[c, k + WU, 0:cy]
                total = total - g * held
            ob[ITERS, c, k] = total
            acc = acc + total * total
        return acc

    acc = loop(cx, close, jnp.zeros((cy, nz), jnp.float32))
    reduce_start(ITERS, [acc])
    for g in range(len(groups)):
        finish(g)
    norm = jnp.sqrt(reduce_end(ITERS, 1)[0])
    entries[(ITERS, ITERS - 1)] = norm
    factor = 1.0 / norm

    def scale(k, carry):
        for c in range(4):
            ob[ITERS, c, k] = ob[ITERS, c, k] * factor
        return carry

    loop(cx, scale)
    final = pltpu.make_async_copy(ob.at[ITERS], basis.at[ITERS], store.at[0, ITERS])
    final.start()
    r = lax.broadcasted_iota(jnp.int32, (ITERS + 1, ITERS), 0)
    c = lax.broadcasted_iota(jnp.int32, (ITERS + 1, ITERS), 1)
    table = jnp.zeros((ITERS + 1, ITERS), jnp.float32)
    for (i, j), value in entries.items():
        table = table + jnp.where(jnp.logical_and(r == i, c == j), value, 0.0)
    hess[...] = table
    for e in range(ITERS + 1):
        red_wait(e, red_send)
    for e in range(ITERS):
        for item in write_out(e):
            item.wait()
    final.wait()


def per_device(slabs, subs, start, wind, reaction, mass):
    _, cx, cy, nz = start.shape
    n = slabs * subs
    rows = cy + HALO
    f32 = jnp.float32

    def field(*lead):
        return pltpu.VMEM((*lead, rows, nz), f32)

    out_shape = (
        jax.ShapeDtypeStruct((ITERS + 1, 4, cx, cy, nz), f32),
        jax.ShapeDtypeStruct((ITERS, 4, cx, cy, nz), f32),
        jax.ShapeDtypeStruct((ITERS + 1, ITERS), f32),
    )
    anywhere = pl.BlockSpec(memory_space=pl.ANY)
    return pl.pallas_call(
        functools.partial(kernel, slabs, subs, cx, cy, nz),
        out_shape=out_shape,
        in_specs=[anywhere] * 4,
        out_specs=(anywhere, anywhere, pl.BlockSpec(memory_space=pltpu.VMEM)),
        scratch_shapes=[
            field(ITERS, cx + 2 * WP),
            field(ITERS, 3, cx + 2 * WU),
            field(ITERS - 1, cx + 2 * WP),
            field(ITERS - 1, 3, cx + 2 * WU),
            field(5, cx + 2 * WC),
            field(9, cx + 2 * WC),
            field(4),
            field(cx + 2 * (WP - 1)),
            field(cx + 2 * WC),
            field(3, cx + 2 * WU),
            field(3, cx + 2),
            pltpu.VMEM((4, cx, cy, nz), f32),
            pltpu.VMEM((ITERS + 1, 4, cx, cy, nz), f32),
            pltpu.VMEM((ITERS, 4, cx, cy, nz), f32),
            pltpu.VMEM((ITERS + 1, n, 1, LANES), f32),
            pltpu.SemaphoreType.DMA((7, 5)),
            pltpu.SemaphoreType.DMA((7, 5)),
            pltpu.SemaphoreType.DMA((ITERS + 1,)),
            pltpu.SemaphoreType.DMA((ITERS + 1,)),
            pltpu.SemaphoreType.DMA((5,)),
            pltpu.SemaphoreType.DMA((2, ITERS + 1)),
        ],
        compiler_params=pltpu.CompilerParams(
            collective_id=0, has_side_effects=True, vmem_limit_bytes=40 * 1024 * 1024
        ),
    )(start, wind, reaction, mass)


def solution(mesh):
    slabs, subs = mesh.shape["slab"], mesh.shape["sub"]
    return jax.shard_map(
        functools.partial(per_device, slabs, subs),
        mesh=mesh,
        in_specs=(
            P(None, "slab", "sub", None),
            P(None, "slab", "sub", None),
            P("slab", "sub", None),
            P("slab", "sub", None),
        ),
        out_specs=(P(None, None, "slab", "sub", None), P(None, None, "slab", "sub", None), P()),
        check_vma=False,
    )
```

time: 418 us -> 79.6 us (0.19)
  blocking collectives: 284 us -> 0 us
  Pallas kernels: 0 us -> 72.2 us
  other arithmetic: 42.8 us -> 0 us
  starting transfers between devices: 34.4 us -> 0 us
  waiting for transfers between devices: 28.3 us -> 0 us
  local copies, waits for them, and re-layouts: 21.4 us -> 6.47 us
    psum x7 -> x0, blocking collectives: 284 us -> none  [the longest x3 122 us: per_device(): norm_next = jnp.sqrt(lax.psum(jnp.sum(image * image), ('slab', 'sub')))]
    pallas_call x0 -> x1, Pallas kernels: none -> 72.2 us  [per_device(): pl.pallas_call(functools.partial(kernel, slabs, subs, cx, cy, nz), out_sh...]
    ppermute x16 -> x0, starting transfers between devices: 34.4 us -> none  [the longest x8 23.7 us: padded_2(): before = lax.ppermute(last, axis, up)]
    ppermute x16 -> x0, waiting for transfers between devices: 28.3 us -> none  [the longest x8 17.4 us: padded_2(): before = lax.ppermute(last, axis, up)]
    another operation x23 -> x0, other arithmetic: 17.4 us -> none
    reduce_sum x7 -> x0, other arithmetic: 11.5 us -> none  [the longest x3 8.42 us: per_device(): norm_next = jnp.sqrt(lax.psum(jnp.sum(image * image), ('slab', 'sub')))]
    scatter x6 -> x0, local copies, waits for them, and re-layouts: 7.94 us -> none  [the longest x3 5.11 us: per_device(): hess = hess.at[:column + 1, column].set(projected)]
    slice x27 -> x0, local copies, waits for them, and re-layouts: 6.1 us -> none  [the longest x15 2.27 us: neighbour_sets(): center[..., 1:]]
  transfers between devices with their start and end apart: 16 -> 0, of which waited for: 9 -> 0; matrix products, arithmetic and copies ran while one was open for 4% -> 0% of each run, Pallas kernels for 0% -> 0%
where the time goes in v1:
time: 79.6 us; the launch traced here: 79.4 us
  Pallas kernels  72.2 us (91%)
  local copies, waits for them, and re-layouts  6.47 us (8%)
    pallas_call x1, Pallas kernels, per_device(): pl.pallas_call(functools.partial(kernel, slabs, subs, cx, cy, nz), out_sh...  72.2 us
    unnamed x11, local copies, waits for them, and re-layouts  6.47 us

profile of v1, /device:TPU:0, one launch (start us, length us, event | category | flops | bytes accessed | tf_op | source)
XLA Modules:
  0.0 79.4 jit_solution(5422836781941411760)
XLA Ops:
  0.6 0.0 copy-start
  0.6 1.0 %copy-done = f32[4,6,16,256]{3,2,1,0:T(8,128)S(1)} copy-done((f32[4,6,16,256]{3,2,1,0:T(8,128)S(1)}, f32[4,6,16,256]{3,2,1,0:T(8,128)}, u32[]{:S(2)}) %copy-start) | copy-done | bytes 393240
  1.6 0.0 copy-start.1
  1.6 1.0 %copy-done.1 = f32[3,6,16,256]{3,2,1,0:T(8,128)S(1)} copy-done((f32[3,6,16,256]{3,2,1,0:T(8,128)S(1)}, f32[3,6,16,256]{3,2,1,0:T(8,128)}, u32[]{:S(2)}) %copy-start.1) | copy-done | bytes 294936
  2.6 0.0 copy-start.2
  2.6 0.9 %copy-done.2 = f32[6,16,256]{2,1,0:T(8,128)S(1)} copy-done((f32[6,16,256]{2,1,0:T(8,128)S(1)}, f32[6,16,256]{2,1,0:T(8,128)}, u32[]{:S(2)}) %copy-start.2) | copy-done | bytes 98328
  3.5 0.0 copy-start.3
  3.5 0.9 %copy-done.3 = f32[6,16,256]{2,1,0:T(8,128)S(1)} copy-done((f32[6,16,256]{2,1,0:T(8,128)S(1)}, f32[6,16,256]{2,1,0:T(8,128)}, u32[]{:S(2)}) %copy-start.3) | copy-done | bytes 98328
  4.4 72.2 %shard_map.67 = (f32[4,4,6,16,256]{4,3,2,1,0:T(8,128)S(1)}, f32[3,4,6,16,256]{4,3,2,1,0:T(8,128)S(1)}, f32[4,3]{1,0:T(4,128)S(1)}) custom-call(f32[4,6,16,256]{3,2,1,0:T(8,128)S(1)} %copy-done, f32[3,6,16,256]{3,2,1,0:T(8,128)S(1)} %copy-done.1, f32[6,16,256]{2,1,0:T(8,128)S(1)} %copy-done.2, f32[6,16,256]{2,1,0:T(8,128)S(1)} %copy-done.3), custom_call_target="tpu_custom_call" | custom-call | tf_op jit(solution)/shard_map/pallas_call | solution.py:458
  76.6 1.1 %copy.10 = f32[4,4,6,16,256]{4,3,2,1,0:T(8,128)} copy(f32[4,4,6,16,256]{4,3,2,1,0:T(8,128)S(1)} %get-tuple-element.6) | data formatting | bytes 3145728
  77.8 1.0 %copy.11 = f32[3,4,6,16,256]{4,3,2,1,0:T(8,128)} copy(f32[3,4,6,16,256]{4,3,2,1,0:T(8,128)S(1)} %get-tuple-element.7) | data formatting | bytes 2359296
  78.8 0.6 copy.12
Async XLA Ops:
  0.6 1.0 %copy-start = (f32[4,6,16,256]{3,2,1,0:T(8,128)S(1)}, f32[4,6,16,256]{3,2,1,0:T(8,128)}, u32[]{:S(2)}) copy-start(f32[4,6,16,256]{3,2,1,0:T(8,128)} %start.1) | copy-start | bytes 1179652
  1.6 1.0 %copy-start.1 = (f32[3,6,16,256]{3,2,1,0:T(8,128)S(1)}, f32[3,6,16,256]{3,2,1,0:T(8,128)}, u32[]{:S(2)}) copy-start(f32[3,6,16,256]{3,2,1,0:T(8,128)} %wind.1) | copy-start | bytes 884740
  2.6 0.9 %copy-start.2 = (f32[6,16,256]{2,1,0:T(8,128)S(1)}, f32[6,16,256]{2,1,0:T(8,128)}, u32[]{:S(2)}) copy-start(f32[6,16,256]{2,1,0:T(8,128)} %reaction.1) | copy-start | bytes 294916
  3.5 0.9 %copy-start.3 = (f32[6,16,256]{2,1,0:T(8,128)S(1)}, f32[6,16,256]{2,1,0:T(8,128)}, u32[]{:S(2)}) copy-start(f32[6,16,256]{2,1,0:T(8,128)} %mass.1) | copy-start | bytes 294916

commit v2 on v1

--- a/solution.py
+++ b/solution.py
@@ -8,7 +8,7 @@
 from jax.sharding import PartitionSpec as P
 
 ITERS = 3
-WP, WU, WC = 5, 2, 3
+WP, WU, WC, WQ = 2, 2, 2, 3
 HALO = 8
 LANES = 128
 MESH = pl.DeviceIdType.MESH
@@ -27,7 +27,7 @@
 def kernel(
     slabs, subs, cx, cy, nz,
     start, wind, reaction, mass, basis, search, hess,
-    xp, xu, vp, vu, raw, co, mk, t1, qq, y0, y1, wl, ob, os_, red,
+    xp, xu, vp, vu, raw, co, mk, t1, qs, y0, y1, wl, ob, os_, red,
     send, recv, red_send, red_recv, load, store,
 ):
     slab, sub = lax.axis_index("slab"), lax.axis_index("sub")
@@ -53,13 +53,17 @@
     barrier = pltpu.get_barrier_semaphore()
 
     def greet(k, carry):
-        other = lax.rem(me + k, n)
+        for other in range(subs):
+            pl.semaphore_signal(
+                barrier, inc=1, device_id=(lax.rem(slab + k, slabs), other), device_id_type=MESH
+            )
+        return carry
+
+    for k in range(1, subs):
         pl.semaphore_signal(
-            barrier, inc=1, device_id=(other // subs, other % subs), device_id_type=MESH
+            barrier, inc=1, device_id=(slab, lax.rem(sub + k, subs)), device_id_type=MESH
         )
-        return carry
-
-    lax.fori_loop(1, n, greet, 0)
+    lax.fori_loop(1, slabs, greet, 0)
 
     def clear(low):
         def inner():
@@ -67,6 +71,9 @@
                 for k in range(WP):
                     at = k if low else WP + cx + k
                     xp[e, at, 0:cy] = jnp.zeros((cy, nz), jnp.float32)
+                for k in range(WQ):
+                    at = k if low else WQ + cx + k
+                    qs[e, at, 0:cy] = jnp.zeros((cy, nz), jnp.float32)
                 for c in range(3):
                     for k in range(WU):
                         at = k if low else WU + cx + k
@@ -97,27 +104,39 @@
     def u_view(e):
         return lambda planes, lines: xu.at[e, :, planes, lines]
 
-    def c_view(planes, lines):
-        return raw.at[:, planes, lines]
-
+    def q_view(e):
+        return lambda planes, lines: qs.at[e, planes, lines]
+
+    def wind_view(planes, lines):
+        return raw.at[pl.ds(0, 3), planes, lines]
+
+    def row_view(i):
+        return lambda planes, lines: raw.at[i, planes, lines]
+
+    every, across = (0, 1, 2, 3, 4), (0, 1, 3, 4)
     groups = [
-        (p_view(0), WP), (u_view(0), WU), (c_view, WC),
-        (p_view(1), WP), (u_view(1), WU), (p_view(2), WP), (u_view(2), WU),
+        (p_view(0), WP, WP, every), (u_view(0), WU, WU, every),
+        (row_view(3), WC, WC, every),
+        (p_view(1), WP, WP, every), (u_view(1), WU, WU, every),
+        (p_view(2), WP, WP, every), (u_view(2), WU, WU, every),
+        (wind_view, WC, 1, every), (row_view(4), WC, 0, (2,)),
+        (q_view(0), WQ, WQ, across), (q_view(1), WQ, WQ, across), (q_view(2), WQ, WQ, across),
     ]
     own_lines = pl.ds(0, cy)
     edge_lines = pl.ds(pl.multiple_of((1 - sub) * (cy - HALO), 8), HALO)
     halo_lines = pl.ds(cy, HALO)
 
     def remote(g, kind):
-        view, w = groups[g]
+        view, base, w, _ = groups[g]
+        end = base + cx
         if kind == 0:
-            src, dst = view(pl.ds(cx, w), own_lines), view(pl.ds(0, w), own_lines)
+            src, dst = view(pl.ds(end - w, w), own_lines), view(pl.ds(base - w, w), own_lines)
             target = {"slab": slab + 1}
         elif kind == 1:
-            src, dst = view(pl.ds(w, w), own_lines), view(pl.ds(w + cx, w), own_lines)
+            src, dst = view(pl.ds(base, w), own_lines), view(pl.ds(end, w), own_lines)
             target = {"slab": slab - 1}
         else:
-            planes = (pl.ds(w, cx), pl.ds(0, w), pl.ds(w + cx, w))[kind - 2]
+            planes = (pl.ds(base, cx), pl.ds(base - w, w), pl.ds(end, w))[kind - 2]
             src, dst = view(planes, edge_lines), view(planes, halo_lines)
             target = {"sub": 1 - sub}
         return pltpu.make_async_remote_copy(
@@ -126,25 +145,33 @@
         )
 
     def begin(g):
-        pl.when(has_right)(lambda: remote(g, 0).start())
-        pl.when(has_left)(lambda: remote(g, 1).start())
-        remote(g, 2).start()
+        kinds = groups[g][3]
+        if 0 in kinds:
+            pl.when(has_right)(lambda: remote(g, 0).start())
+            pl.when(has_left)(lambda: remote(g, 1).start())
+        if 2 in kinds:
+            remote(g, 2).start()
 
     def forward(g):
-        pl.when(has_left)(lambda: remote(g, 0).wait_recv())
-        remote(g, 3).start()
-        pl.when(has_right)(lambda: remote(g, 1).wait_recv())
-        remote(g, 4).start()
+        if 0 in groups[g][3]:
+            pl.when(has_left)(lambda: remote(g, 0).wait_recv())
+            remote(g, 3).start()
+            pl.when(has_right)(lambda: remote(g, 1).wait_recv())
+            remote(g, 4).start()
 
     def arrive(g):
-        for kind in (2, 3, 4):
-            remote(g, kind).wait_recv()
+        for kind in groups[g][3]:
+            if kind >= 2:
+                remote(g, kind).wait_recv()
 
     def finish(g):
-        pl.when(has_right)(lambda: remote(g, 0).wait_send())
-        pl.when(has_left)(lambda: remote(g, 1).wait_send())
-        for kind in (2, 3, 4):
-            remote(g, kind).wait_send()
+        for kind in groups[g][3]:
+            if kind == 0:
+                pl.when(has_right)(lambda: remote(g, 0).wait_send())
+            elif kind == 1:
+                pl.when(has_left)(lambda: remote(g, 1).wait_send())
+            else:
+                remote(g, kind).wait_send()
 
     lane = lax.broadcasted_iota(jnp.int32, (1, LANES), 1)
 
@@ -154,16 +181,22 @@
             line = line + jnp.where(lane == i, jnp.sum(fold(part), keepdims=True), 0.0)
         red[e, me] = line
 
-        def push(k, carry):
-            other = lax.rem(me + k, n)
+        def tell(at, core):
             pltpu.make_async_remote_copy(
                 src_ref=red.at[e, me], dst_ref=red.at[e, me],
                 send_sem=red_send.at[e], recv_sem=red_recv.at[e],
-                device_id=(other // subs, other % subs), device_id_type=MESH,
+                device_id=(at, core), device_id_type=MESH,
             ).start()
-            return carry
-
-        lax.fori_loop(1, n, push, 0)
+
+        def push(k, carry):
+            at = lax.rem(slab + k, slabs)
+            for core in range(subs):
+                tell(at, core)
+            return carry
+
+        lax.fori_loop(1, slabs, push, 0)
+        for k in range(1, subs):
+            tell(slab, lax.rem(sub + k, subs))
 
     def red_wait(e, sem):
         block = red.at[e, pl.ds(0, n - 1)]
@@ -230,19 +263,19 @@
 
         loop(cx + 2 * (WP - 1), body)
 
-    def schur():
+    def schur(qq):
         def body(k, carry):
             here = t1[k + 1]
-            off = off_diagonal(t1[k], turn(here), t1[k + 2], k)
-            qq[k] = (off - co[6, k] * here) * co[8, k]
-            return carry
-
-        loop(cx + 2 * WC, body)
-
-    def velocity_first(u):
+            off = off_diagonal(t1[k], turn(here), t1[k + 2], k + WC)
+            qq[k + WQ] = (off - co[6, k + WC] * here) * co[8, k + WC]
+            return carry
+
+        loop(cx, body)
+
+    def velocity_first(qq, u):
         def body(k, carry):
             yp, ym, zp, zm = masked(qq[k + 1])
-            scale = co[7, k + 1]
+            scale = co[7, k]
             y0[0, k] = (u[0, k] - 0.5 * (qq[k + 2] - qq[k])) * scale
             y0[1, k] = (u[1, k] - 0.5 * (yp - ym)) * scale
             y0[2, k] = (u[2, k] - 0.5 * (zp - zm)) * scale
@@ -252,19 +285,19 @@
 
     def velocity_second():
         def body(k, carry):
-            scale = co[7, k + 2]
+            scale = co[7, k + 1]
             for c in range(3):
                 here = y0[c, k + 1]
-                off = off_diagonal(y0[c, k], turn(here), y0[c, k + 2], k + 2)
+                off = off_diagonal(y0[c, k], turn(here), y0[c, k + 2], k + 1)
                 y1[c, k] = here + off * scale
             return carry
 
         loop(cx + 2, body)
 
-    def image(e, vectors):
+    def image(e, qq, vectors):
         def body(k, acc):
-            q = qq[k + WC]
-            qa, qb = qq[k + WC + 1], qq[k + WC - 1]
+            q = qq[k + WQ]
+            qa, qb = qq[k + WQ + 1], qq[k + WQ - 1]
             yp, ym, zp, zm = masked(q)
             grads = (0.5 * (qa - qb), 0.5 * (yp - ym), 0.5 * (zp - zm))
             low = 0.5 * ((qa + qb) + (yp + ym) + (zp + zm)) - 3.0 * q
@@ -330,7 +363,8 @@
     begin(0)
     for item in loads[2:]:
         item.wait()
-    begin(2)
+    for g in (2, 7, 8):
+        begin(g)
     loads[1].wait()
     begin(1)
     forward(0)
@@ -340,21 +374,24 @@
     inverses = []
     entries = {}
     first_guess(vectors[0][0])
-    forward(2)
-    arrive(2)
+    for g in (2, 7):
+        forward(g)
+    for g in (2, 7, 8):
+        arrive(g)
     coefficients()
     for e in range(ITERS):
         p, u = vectors[e]
         p_group, u_group = ((0, 1), (3, 4), (5, 6))[e]
         if e > 0:
             first_guess(p)
-        schur()
-        if e == 0:
-            forward(u_group)
-            arrive(u_group)
-        else:
-            forward(u_group)
-            arrive(u_group)
+        qq = qs.at[e]
+        schur(qq)
+        begin(9 + e)
+        if e > 0:
+            results(e - 1, vectors[e - 1], inverses[e - 1])
+        forward(u_group)
+        arrive(u_group)
+        if e > 0:
 
             def form_u(k, carry, e=e):
                 for c in range(3):
@@ -365,9 +402,11 @@
                 return carry
 
             loop(cx + 2 * WU, form_u)
-        velocity_first(u)
+        forward(9 + e)
+        arrive(9 + e)
+        velocity_first(qq, u)
         velocity_second()
-        acc = image(e, vectors)
+        acc = image(e, qq, vectors)
         reduce_start(e, acc)
         if e + 1 < ITERS:
             begin(p_group + 3 if e == 0 else 5)
@@ -383,7 +422,6 @@
             h = sums[i + 1] * inverses[i] * factor
             entries[(i, e)] = h
             weights.append(h * inverses[i])
-        results(e, vectors[e], factor)
         if e + 1 < ITERS:
             g_p = (3, 5)[e]
             forward(g_p)
@@ -412,6 +450,7 @@
 
     acc = loop(cx, close, jnp.zeros((cy, nz), jnp.float32))
     reduce_start(ITERS, [acc])
+    results(ITERS - 1, vectors[ITERS - 1], inverses[ITERS - 1])
     for g in range(len(groups)):
         finish(g)
     norm = jnp.sqrt(reduce_end(ITERS, 1)[0])
@@ -458,7 +497,7 @@
     return pl.pallas_call(
         functools.partial(kernel, slabs, subs, cx, cy, nz),
         out_shape=out_shape,
-        in_specs=[anywhere] * 4,
+        in_specs=[pl.BlockSpec(memory_space=pltpu.HBM)] * 4,
         out_specs=(anywhere, anywhere, pl.BlockSpec(memory_space=pltpu.VMEM)),
         scratch_shapes=[
             field(ITERS, cx + 2 * WP),
@@ -469,15 +508,15 @@
             field(9, cx + 2 * WC),
             field(4),
             field(cx + 2 * (WP - 1)),
-            field(cx + 2 * WC),
+            field(ITERS, cx + 2 * WQ),
             field(3, cx + 2 * WU),
             field(3, cx + 2),
             pltpu.VMEM((4, cx, cy, nz), f32),
             pltpu.VMEM((ITERS + 1, 4, cx, cy, nz), f32),
             pltpu.VMEM((ITERS, 4, cx, cy, nz), f32),
             pltpu.VMEM((ITERS + 1, n, 1, LANES), f32),
-            pltpu.SemaphoreType.DMA((7, 5)),
-            pltpu.SemaphoreType.DMA((7, 5)),
+            pltpu.SemaphoreType.DMA((12, 5)),
+            pltpu.SemaphoreType.DMA((12, 5)),
             pltpu.SemaphoreType.DMA((ITERS + 1,)),
             pltpu.SemaphoreType.DMA((ITERS + 1,)),
             pltpu.SemaphoreType.DMA((5,)),

time: 79.6 us -> 75.2 us (0.945)
  Pallas kernels: 72.2 us -> 67.8 us
    pallas_call x1, Pallas kernels: 72.2 us -> 67.8 us  [per_device(): pl.pallas_call(functools.partial(kernel, slabs, subs, cx, cy, nz), out_sh...]
where the time goes in v2:
time: 75.2 us; the launch traced here: 74.9 us
  Pallas kernels  67.8 us (90%)
  local copies, waits for them, and re-layouts  6.47 us (9%)
    pallas_call x1, Pallas kernels, per_device(): pl.pallas_call(functools.partial(kernel, slabs, subs, cx, cy, nz), out_sh...  67.8 us
    unnamed x11, local copies, waits for them, and re-layouts  6.47 us

profile of v2, /device:TPU:0, one launch (start us, length us, event | category | flops | bytes accessed | tf_op | source)
XLA Modules:
  0.0 74.9 jit_solution(8882438670692127796)
XLA Ops:
  0.6 0.0 copy-start
  0.6 1.0 %copy-done = f32[4,6,16,256]{3,2,1,0:T(8,128)S(1)} copy-done((f32[4,6,16,256]{3,2,1,0:T(8,128)S(1)}, f32[4,6,16,256]{3,2,1,0:T(8,128)}, u32[]{:S(2)}) %copy-start) | copy-done | bytes 393240
  1.6 0.0 copy-start.1
  1.6 1.0 %copy-done.1 = f32[3,6,16,256]{3,2,1,0:T(8,128)S(1)} copy-done((f32[3,6,16,256]{3,2,1,0:T(8,128)S(1)}, f32[3,6,16,256]{3,2,1,0:T(8,128)}, u32[]{:S(2)}) %copy-start.1) | copy-done | bytes 294936
  2.6 0.0 copy-start.2
  2.6 0.9 %copy-done.2 = f32[6,16,256]{2,1,0:T(8,128)S(1)} copy-done((f32[6,16,256]{2,1,0:T(8,128)S(1)}, f32[6,16,256]{2,1,0:T(8,128)}, u32[]{:S(2)}) %copy-start.2) | copy-done | bytes 98328
  3.5 0.0 copy-start.3
  3.5 0.9 %copy-done.3 = f32[6,16,256]{2,1,0:T(8,128)S(1)} copy-done((f32[6,16,256]{2,1,0:T(8,128)S(1)}, f32[6,16,256]{2,1,0:T(8,128)}, u32[]{:S(2)}) %copy-start.3) | copy-done | bytes 98328
  4.4 67.8 %shard_map.67 = (f32[4,4,6,16,256]{4,3,2,1,0:T(8,128)S(1)}, f32[3,4,6,16,256]{4,3,2,1,0:T(8,128)S(1)}, f32[4,3]{1,0:T(4,128)S(1)}) custom-call(f32[4,6,16,256]{3,2,1,0:T(8,128)S(1)} %copy-done, f32[3,6,16,256]{3,2,1,0:T(8,128)S(1)} %copy-done.1, f32[6,16,256]{2,1,0:T(8,128)S(1)} %copy-done.2, f32[6,16,256]{2,1,0:T(8,128)S(1)} %copy-done.3), custom_call_target="tpu_custom_call" | custom-call | tf_op jit(solution)/shard_map/pallas_call | solution.py:497
  72.2 1.1 %copy.10 = f32[4,4,6,16,256]{4,3,2,1,0:T(8,128)} copy(f32[4,4,6,16,256]{4,3,2,1,0:T(8,128)S(1)} %get-tuple-element.6) | data formatting | bytes 3145728
  73.4 1.0 %copy.11 = f32[3,4,6,16,256]{4,3,2,1,0:T(8,128)} copy(f32[3,4,6,16,256]{4,3,2,1,0:T(8,128)S(1)} %get-tuple-element.7) | data formatting | bytes 2359296
  74.4 0.6 copy.12
Async XLA Ops:
  0.6 1.0 %copy-start = (f32[4,6,16,256]{3,2,1,0:T(8,128)S(1)}, f32[4,6,16,256]{3,2,1,0:T(8,128)}, u32[]{:S(2)}) copy-start(f32[4,6,16,256]{3,2,1,0:T(8,128)} %start.1) | copy-start | bytes 1179652
  1.6 1.0 %copy-start.1 = (f32[3,6,16,256]{3,2,1,0:T(8,128)S(1)}, f32[3,6,16,256]{3,2,1,0:T(8,128)}, u32[]{:S(2)}) copy-start(f32[3,6,16,256]{3,2,1,0:T(8,128)} %wind.1) | copy-start | bytes 884740
  2.6 0.9 %copy-start.2 = (f32[6,16,256]{2,1,0:T(8,128)S(1)}, f32[6,16,256]{2,1,0:T(8,128)}, u32[]{:S(2)}) copy-start(f32[6,16,256]{2,1,0:T(8,128)} %reaction.1) | copy-start | bytes 294916
  3.5 0.9 %copy-start.3 = (f32[6,16,256]{2,1,0:T(8,128)S(1)}, f32[6,16,256]{2,1,0:T(8,128)}, u32[]{:S(2)}) copy-start(f32[6,16,256]{2,1,0:T(8,128)} %mass.1) | copy-start | bytes 294916

commit v3 on v2

--- a/solution.py
+++ b/solution.py
@@ -8,6 +8,7 @@
 from jax.sharding import PartitionSpec as P
 
 ITERS = 3
+UNROLL = 3
 WP, WU, WC, WQ = 2, 2, 2, 3
 HALO = 8
 LANES = 128
@@ -159,9 +160,9 @@
             pl.when(has_right)(lambda: remote(g, 1).wait_recv())
             remote(g, 4).start()
 
-    def arrive(g):
+    def arrive(g, kinds=(2, 3, 4)):
         for kind in groups[g][3]:
-            if kind >= 2:
+            if kind in kinds:
                 remote(g, kind).wait_recv()
 
     def finish(g):
@@ -226,8 +227,20 @@
         total = total + (co[2, k] * yp + co[3, k] * ym)
         return total + (co[4, k] * zp + co[5, k] * zm)
 
-    def loop(count, body, init=0):
-        return lax.fori_loop(0, count, body, init)
+    def loop(count, body, init=0, low=0):
+        step = max(u for u in range(1, UNROLL + 1) if count % u == 0)
+
+        def several(k, carry):
+            for i in range(step):
+                carry = body(low + k * step + i, carry)
+            return carry
+
+        return lax.fori_loop(0, count // step, several, init)
+
+    def spans(spans_of, body):
+        for low, high in spans_of:
+            if high > low:
+                loop(high - low, body, low=low)
 
     def inside(k, w):
         at = slab * cx + k - w
@@ -272,7 +285,7 @@
 
         loop(cx, body)
 
-    def velocity_first(qq, u):
+    def velocity_first(qq, u, where):
         def body(k, carry):
             yp, ym, zp, zm = masked(qq[k + 1])
             scale = co[7, k]
@@ -281,9 +294,9 @@
             y0[2, k] = (u[2, k] - 0.5 * (zp - zm)) * scale
             return carry
 
-        loop(cx + 2 * WU, body)
-
-    def velocity_second():
+        spans(where, body)
+
+    def velocity_second(where):
         def body(k, carry):
             scale = co[7, k + 1]
             for c in range(3):
@@ -292,7 +305,7 @@
                 y1[c, k] = here + off * scale
             return carry
 
-        loop(cx + 2, body)
+        spans(where, body)
 
     def image(e, qq, vectors):
         def body(k, acc):
@@ -389,8 +402,10 @@
         begin(9 + e)
         if e > 0:
             results(e - 1, vectors[e - 1], inverses[e - 1])
-        forward(u_group)
-        arrive(u_group)
+        end_u, end_1 = cx + 2 * WU, cx + 2
+        deep = min(3, end_1 // 2)
+        inner = (WU + 1, WU + cx - 1)
+        arrive(u_group, (2,))
         if e > 0:
 
             def form_u(k, carry, e=e):
@@ -401,11 +416,17 @@
                     u[c, k] = total
                 return carry
 
-            loop(cx + 2 * WU, form_u)
+            spans([(WU, WU + cx)], form_u)
+        velocity_first(qq, u, [inner])
+        velocity_second([(deep, end_1 - deep)])
+        forward(u_group)
         forward(9 + e)
+        arrive(u_group, (3, 4))
+        if e > 0:
+            spans([(0, WU), (WU + cx, end_u)], form_u)
         arrive(9 + e)
-        velocity_first(qq, u)
-        velocity_second()
+        velocity_first(qq, u, [(0, inner[0]), (inner[1], end_u)])
+        velocity_second([(0, deep), (end_1 - deep, end_1)])
         acc = image(e, qq, vectors)
         reduce_start(e, acc)
         if e + 1 < ITERS:
@@ -523,7 +544,7 @@
             pltpu.SemaphoreType.DMA((2, ITERS + 1)),
         ],
         compiler_params=pltpu.CompilerParams(
-            collective_id=0, has_side_effects=True, vmem_limit_bytes=40 * 1024 * 1024
+            collective_id=0, has_side_effects=True, vmem_limit_bytes=63_900_000
         ),
     )(start, wind, reaction, mass)
 

time: 75.2 us -> 68.5 us (0.911)
  Pallas kernels: 67.8 us -> 63.3 us
  local copies, waits for them, and re-layouts: 6.47 us -> 4.41 us
    pallas_call x1, Pallas kernels: 67.8 us -> 63.3 us  [per_device(): pl.pallas_call(functools.partial(kernel, slabs, subs, cx, cy, nz), out_sh...]
    unnamed x11 -> x7, local copies, waits for them, and re-layouts: 6.47 us -> 4.41 us
where the time goes in v3:
time: 68.5 us; the launch traced here: 68.4 us
  Pallas kernels  63.3 us (92%)
  local copies, waits for them, and re-layouts  4.41 us (6%)
    pallas_call x1, Pallas kernels, per_device(): pl.pallas_call(functools.partial(kernel, slabs, subs, cx, cy, nz), out_sh...  63.3 us
    unnamed x7, local copies, waits for them, and re-layouts  4.41 us

profile of v3, /device:TPU:0, one launch (start us, length us, event | category | flops | bytes accessed | tf_op | source)
XLA Modules:
  0.0 68.4 jit_solution(16450145052220415574)
XLA Ops:
  0.6 63.3 %shard_map.67 = (f32[4,4,6,16,256]{4,3,2,1,0:T(8,128)}, f32[3,4,6,16,256]{4,3,2,1,0:T(8,128)}, f32[4,3]{1,0:T(4,128)}) custom-call(f32[4,6,16,256]{3,2,1,0:T(8,128)} %start.1, f32[3,6,16,256]{3,2,1,0:T(8,128)} %wind.1, f32[6,16,256]{2,1,0:T(8,128)} %reaction.1, f32[6,16,256]{2,1,0:T(8,128)} %mass.1), custom_call_target="tpu_custom_call" | custom-call | tf_op jit(solution)/shard_map/pallas_call | solution.py:518
  63.9 0.0 copy-start
  64.0 2.8 %copy.10 = f32[4,4,6,16,256]{4,3,2,1,0:T(8,128)} copy(f32[4,4,6,16,256]{4,3,2,1,0:T(8,128)} %get-tuple-element.6) | data formatting | bytes 3145728
  66.8 0.0 copy-done
  66.8 0.0 copy-start.1
  66.8 1.0 %copy.11 = f32[3,4,6,16,256]{4,3,2,1,0:T(8,128)} copy(f32[3,4,6,16,256]{4,3,2,1,0:T(8,128)S(1)} %copy-done) | data formatting | bytes 2359296
  67.8 0.0 copy-done.1
  67.8 0.6 copy.12
Async XLA Ops:
  63.9 2.8 %copy-start = (f32[3,4,6,16,256]{4,3,2,1,0:T(8,128)S(1)}, f32[3,4,6,16,256]{4,3,2,1,0:T(8,128)}, u32[]{:S(2)}) copy-start(f32[3,4,6,16,256]{4,3,2,1,0:T(8,128)} %get-tuple-element.7) | copy-start | bytes 3538948
  66.8 1.0 %copy-start.1 = (f32[4,3]{1,0:T(4,128)S(1)}, f32[4,3]{1,0:T(4,128)}, u32[]{:S(2)}) copy-start(f32[4,3]{1,0:T(4,128)} %get-tuple-element.8) | copy-start | bytes 148

commit v4 on v3

--- a/solution.py
+++ b/solution.py
@@ -145,8 +145,8 @@
             device_id=target, device_id_type=MESH,
         )
 
-    def begin(g):
-        kinds = groups[g][3]
+    def begin(g, chosen=(0, 1, 2)):
+        kinds = [kind for kind in groups[g][3] if kind in chosen]
         if 0 in kinds:
             pl.when(has_right)(lambda: remote(g, 0).start())
             pl.when(has_left)(lambda: remote(g, 1).start())
@@ -246,7 +246,7 @@
         at = slab * cx + k - w
         return jnp.logical_and(at >= 0, at < slabs * cx)
 
-    def coefficients():
+    def coefficients(where):
         def body(k, carry):
             ok = jnp.where(inside(k, WC), 1.0, 0.0)
             keep = jnp.full((rows, nz), ok) > 0.5
@@ -263,7 +263,7 @@
             co[8, k] = jnp.where(keep, 1.0 / raw[4, k], 0.0)
             return carry
 
-        loop(cx + 2 * WC, body)
+        spans(where, body)
 
     def first_guess(p):
         def body(k, carry):
@@ -349,7 +349,15 @@
             return tuple(acc)
 
         zero = jnp.zeros((cy, nz), jnp.float32)
-        return loop(cx, body, (zero,) * (e + 2))
+        acc = (zero,) * (e + 2)
+        acc = loop(WP, body, acc)
+        acc = loop(WP, body, acc, low=cx - WP)
+        if e + 1 < ITERS:
+            begin((3, 5)[e], (0, 1))
+        acc = loop(cx - 2 * WP, body, acc, low=WP)
+        if e + 1 < ITERS:
+            begin((3, 5)[e], (2,))
+        return acc
 
     def write_out(e):
         return (
@@ -377,9 +385,14 @@
     for item in loads[2:]:
         item.wait()
     for g in (2, 7, 8):
-        begin(g)
+        begin(g, (2,))
     loads[1].wait()
     begin(1)
+    for g in (2, 7):
+        begin(g, (0, 1))
+    for g in (2, 7, 8):
+        arrive(g, (2,))
+    coefficients([(WC, WC + cx)])
     forward(0)
     arrive(0)
 
@@ -387,11 +400,6 @@
     inverses = []
     entries = {}
     first_guess(vectors[0][0])
-    for g in (2, 7):
-        forward(g)
-    for g in (2, 7, 8):
-        arrive(g)
-    coefficients()
     for e in range(ITERS):
         p, u = vectors[e]
         p_group, u_group = ((0, 1), (3, 4), (5, 6))[e]
@@ -420,6 +428,12 @@
         velocity_first(qq, u, [inner])
         velocity_second([(deep, end_1 - deep)])
         forward(u_group)
+        if e == 0:
+            for g in (2, 7):
+                forward(g)
+            for g in (2, 7):
+                arrive(g, (3, 4))
+            coefficients([(0, WC), (WC + cx, cx + 2 * WC)])
         forward(9 + e)
         arrive(u_group, (3, 4))
         if e > 0:
@@ -430,7 +444,6 @@
         acc = image(e, qq, vectors)
         reduce_start(e, acc)
         if e + 1 < ITERS:
-            begin(p_group + 3 if e == 0 else 5)
             begin(u_group + 3 if e == 0 else 6)
         sums = reduce_end(e, e + 2)
         norm = jnp.sqrt(sums[0])

time: 68.5 us -> 66.8 us (0.975)
  Pallas kernels: 63.3 us -> 61.6 us
    pallas_call x1, Pallas kernels: 63.3 us -> 61.6 us  [per_device(): pl.pallas_call(functools.partial(kernel, slabs, subs, cx, cy, nz), out_sh...]
where the time goes in v4:
time: 66.8 us; the launch traced here: 66.7 us
  Pallas kernels  61.6 us (92%)
  local copies, waits for them, and re-layouts  4.41 us (7%)
    pallas_call x1, Pallas kernels, per_device(): pl.pallas_call(functools.partial(kernel, slabs, subs, cx, cy, nz), out_sh...  61.6 us
    unnamed x7, local copies, waits for them, and re-layouts  4.41 us

profile of v4, /device:TPU:0, one launch (start us, length us, event | category | flops | bytes accessed | tf_op | source)
XLA Modules:
  0.0 66.7 jit_solution(9226176609088218981)
XLA Ops:
  0.6 61.6 %shard_map.67 = (f32[4,4,6,16,256]{4,3,2,1,0:T(8,128)}, f32[3,4,6,16,256]{4,3,2,1,0:T(8,128)}, f32[4,3]{1,0:T(4,128)}) custom-call(f32[4,6,16,256]{3,2,1,0:T(8,128)} %start.1, f32[3,6,16,256]{3,2,1,0:T(8,128)} %wind.1, f32[6,16,256]{2,1,0:T(8,128)} %reaction.1, f32[6,16,256]{2,1,0:T(8,128)} %mass.1), custom_call_target="tpu_custom_call" | custom-call | tf_op jit(solution)/shard_map/pallas_call | solution.py:531
  62.3 0.0 copy-start
  62.3 2.8 %copy.10 = f32[4,4,6,16,256]{4,3,2,1,0:T(8,128)} copy(f32[4,4,6,16,256]{4,3,2,1,0:T(8,128)} %get-tuple-element.6) | data formatting | bytes 3145728
  65.1 0.0 copy-done
  65.1 0.0 copy-start.1
  65.1 1.0 %copy.11 = f32[3,4,6,16,256]{4,3,2,1,0:T(8,128)} copy(f32[3,4,6,16,256]{4,3,2,1,0:T(8,128)S(1)} %copy-done) | data formatting | bytes 2359296
  66.1 0.0 copy-done.1
  66.1 0.6 copy.12
Async XLA Ops:
  62.3 2.8 %copy-start = (f32[3,4,6,16,256]{4,3,2,1,0:T(8,128)S(1)}, f32[3,4,6,16,256]{4,3,2,1,0:T(8,128)}, u32[]{:S(2)}) copy-start(f32[3,4,6,16,256]{4,3,2,1,0:T(8,128)} %get-tuple-element.7) | copy-start | bytes 3538948
  65.1 1.0 %copy-start.1 = (f32[4,3]{1,0:T(4,128)S(1)}, f32[4,3]{1,0:T(4,128)}, u32[]{:S(2)}) copy-start(f32[4,3]{1,0:T(4,128)} %get-tuple-element.8) | copy-start | bytes 148

commit v5 on v4

--- a/solution.py
+++ b/solution.py
@@ -8,7 +8,7 @@
 from jax.sharding import PartitionSpec as P
 
 ITERS = 3
-UNROLL = 3
+UNROLL = 5
 WP, WU, WC, WQ = 2, 2, 2, 3
 HALO = 8
 LANES = 128

time: 66.8 us -> 66.5 us (level)
  no operation moved by 1% of the time
where the time goes in v5:
time: 66.5 us; the launch traced here: 66.4 us
  Pallas kernels  61.3 us (92%)
  local copies, waits for them, and re-layouts  4.41 us (7%)
    pallas_call x1, Pallas kernels, per_device(): pl.pallas_call(functools.partial(kernel, slabs, subs, cx, cy, nz), out_sh...  61.3 us
    unnamed x7, local copies, waits for them, and re-layouts  4.41 us

profile of v5, /device:TPU:0, one launch (start us, length us, event | category | flops | bytes accessed | tf_op | source)
XLA Modules:
  0.0 66.4 jit_solution(2283616478409074870)
XLA Ops:
  0.6 61.3 %shard_map.67 = (f32[4,4,6,16,256]{4,3,2,1,0:T(8,128)}, f32[3,4,6,16,256]{4,3,2,1,0:T(8,128)}, f32[4,3]{1,0:T(4,128)}) custom-call(f32[4,6,16,256]{3,2,1,0:T(8,128)} %start.1, f32[3,6,16,256]{3,2,1,0:T(8,128)} %wind.1, f32[6,16,256]{2,1,0:T(8,128)} %reaction.1, f32[6,16,256]{2,1,0:T(8,128)} %mass.1), custom_call_target="tpu_custom_call" | custom-call | tf_op jit(solution)/shard_map/pallas_call | solution.py:531
  61.9 0.0 copy-start
  62.0 2.8 %copy.10 = f32[4,4,6,16,256]{4,3,2,1,0:T(8,128)} copy(f32[4,4,6,16,256]{4,3,2,1,0:T(8,128)} %get-tuple-element.6) | data formatting | bytes 3145728
  64.8 0.0 copy-done
  64.8 0.0 copy-start.1
  64.8 1.0 %copy.11 = f32[3,4,6,16,256]{4,3,2,1,0:T(8,128)} copy(f32[3,4,6,16,256]{4,3,2,1,0:T(8,128)S(1)} %copy-done) | data formatting | bytes 2359296
  65.8 0.0 copy-done.1
  65.8 0.6 copy.12
Async XLA Ops:
  61.9 2.8 %copy-start = (f32[3,4,6,16,256]{4,3,2,1,0:T(8,128)S(1)}, f32[3,4,6,16,256]{4,3,2,1,0:T(8,128)}, u32[]{:S(2)}) copy-start(f32[3,4,6,16,256]{4,3,2,1,0:T(8,128)} %get-tuple-element.7) | copy-start | bytes 3538948
  64.8 1.0 %copy-start.1 = (f32[4,3]{1,0:T(4,128)S(1)}, f32[4,3]{1,0:T(4,128)}, u32[]{:S(2)}) copy-start(f32[4,3]{1,0:T(4,128)} %get-tuple-element.8) | copy-start | bytes 148
